TPU v7x, 32 devices: a whole 2x2x4 slice. The times are simulated.
32 devices in a mesh: frame: 4 (over z), space: 8 (over y, x, core).
Axes of the slice: x: 2, y: 2, z: 4, core: 2. Of those that a mesh axis runs over, the one named last changes fastest.
Arguments:
- tokens: bfloat16 [32, 152, 1024], P('space', 'frame'), may hold values from -16 to 16
- tube_count: int32 [8], P('space'), may hold values from 1 to 4, as said below
- ln_gain: float32 [1024], replicated, may hold values from 0.25 to 1.75
- ln_bias: float32 [1024], replicated, may hold values from -3 to 3
- w_qkv: bfloat16 [1024, 1536], replicated, may hold values from -1.5 to 1.5
- w_out: bfloat16 [512, 1024], replicated, may hold values from -0.25 to 0.25
Outputs:
- mixed: bfloat16 [32, 152, 1024], P('space', 'frame')
Inputs may be any that keep to these rules, and one draw needn't show every extreme that they name: tube_count[s] is how many of the 4 slots of space index s hold visible tubes; they are the first ones. Some index has all 4, some only 1.
All inputs are finite; a program needn't handle non-finite values.
Results may differ from a plain program's by a relative error of at most 0.005.
Values may be sent and summed in bfloat16 or wider, within the bound.
A program may use at most 128 MiB of HBM per device.

v0:
```python
import jax
import jax.numpy as jnp
from jax import lax
from jax.sharding import PartitionSpec as P

HEADS = 8


EPSILON = 1e-06
NEG_FILL = -1e30


def layer_norm(flat, ln_gain, ln_bias):
    values32 = flat.astype(jnp.float32)
    center = values32 - jnp.mean(values32, axis=-1, keepdims=True)
    spread = jnp.mean(center * center, axis=-1, keepdims=True)
    return (center * lax.rsqrt(spread + EPSILON) * ln_gain + ln_bias).astype(jnp.bfloat16)


def live_mask(counts, slots_dev, time_dev):
    slot_ids = jnp.arange(slots_dev)[None, :, None]
    marks = jnp.broadcast_to(
        slot_ids < counts[:, None, None], (counts.shape[0], slots_dev, time_dev)
    )
    return marks.reshape(-1)


def attend(carry, query_heads, key_block, value_block, live_keys, scaling):
    best_now, total_now, accum = carry
    heads = query_heads.shape[1]
    key_heads = key_block.reshape(key_block.shape[0], heads, -1)
    value_heads = value_block.reshape(value_block.shape[0], heads, -1)
    scores = (
        jnp.einsum("qhd,khd->hqk", query_heads, key_heads, preferred_element_type=jnp.float32)
        * scaling
    )
    scores = jnp.where(live_keys[None, None, :], scores, NEG_FILL)
    best_next = jnp.maximum(best_now, jnp.max(scores, axis=-1))
    fading = jnp.exp(best_now - best_next)
    weights = jnp.exp(scores - best_next[..., None])
    total_next = total_now * fading + jnp.sum(weights, axis=-1)
    accum = accum * fading[..., None] + jnp.einsum(
        "hqk,khd->hqd",
        weights.astype(jnp.bfloat16),
        value_heads,
        preferred_element_type=jnp.float32,
    )
    return (best_next, total_next, accum)


def make_fold(query_heads, vis_dev, time_dev, scaling):
    rows_dev = vis_dev * time_dev

    def fold_masked(carry, piece, start):
        key_all, value_all, count_all = piece
        width_in = key_all.shape[1]
        shards = count_all.shape[0]
        group = 1
        for unused_bit in range(6):
            if shards % (group * 2) == 0 and group * rows_dev < 2048:
                group = group * 2
        blocks = shards // group
        key_groups = key_all.reshape(blocks, group * rows_dev, width_in)
        value_groups = value_all.reshape(blocks, group * rows_dev, width_in)
        count_groups = count_all.reshape(blocks, group)

        def step_group(state, item):
            key_group, value_group, count_group = item
            marks = live_mask(count_group, vis_dev, time_dev)
            return (attend(state, query_heads, key_group, value_group, marks, scaling), None)

        carry, unused = lax.scan(step_group, carry, (key_groups, value_groups, count_groups))
        return carry

    return fold_masked


def start_state(heads, rows, head_size):
    return (
        jnp.full((heads, rows), NEG_FILL, jnp.float32),
        jnp.zeros((heads, rows), jnp.float32),
        jnp.zeros((heads, rows, head_size), jnp.float32),
    )


def on_device(tokens, tube_count, ln_gain, ln_bias, w_qkv, w_out):
    vis_dev, time_dev, width = tokens.shape
    rows_dev = vis_dev * time_dev
    inner = w_out.shape[0]
    head_size = inner // HEADS
    flat = tokens.reshape(rows_dev, width)
    normed = layer_norm(flat, ln_gain, ln_bias)
    projected = jnp.dot(normed, w_qkv, preferred_element_type=jnp.float32).astype(jnp.bfloat16)
    scaling = head_size ** (-0.5)
    frames = lax.axis_size("frame")
    local_heads = HEADS // frames
    stacked = projected.reshape(rows_dev, 3, HEADS, head_size)
    regrouped = lax.all_to_all(stacked, "frame", split_axis=2, concat_axis=0, tiled=True)
    all_rows = regrouped.shape[0]
    query_local = regrouped[:, 0]
    key_local = regrouped[:, 1].reshape(all_rows, local_heads * head_size)
    value_local = regrouped[:, 2].reshape(all_rows, local_heads * head_size)
    counts_rep = jnp.tile(tube_count, frames)
    fold_fn = make_fold(query_local, vis_dev, time_dev, scaling)
    state = fold_fn(
        start_state(local_heads, all_rows, head_size),
        (
            lax.all_gather(key_local, "space", axis=0, tiled=True),
            lax.all_gather(value_local, "space", axis=0, tiled=True),
            lax.all_gather(counts_rep, "space", axis=0, tiled=True),
        ),
        jnp.int32(0),
    )
    best_final, total_final, accum_final = state
    attended = (accum_final / total_final[..., None]).astype(jnp.bfloat16)
    attended = jnp.transpose(attended, (1, 0, 2))
    returned = lax.all_to_all(attended, "frame", split_axis=0, concat_axis=1, tiled=True)
    attended = returned.reshape(rows_dev, inner)
    mixed = flat.astype(jnp.float32) + jnp.dot(attended, w_out, preferred_element_type=jnp.float32)
    own_live = live_mask(tube_count, vis_dev, time_dev)
    mixed = jnp.where(own_live[:, None], mixed, 0.0)
    return mixed.astype(jnp.bfloat16).reshape(vis_dev, time_dev, width)


def solution(mesh):
    in_specs = (P("space", "frame", None), P("space"), P(), P(), P(), P())
    out_specs = P("space", "frame", None)
    return jax.shard_map(
        on_device, mesh=mesh, in_specs=in_specs, out_specs=out_specs, check_vma=False
    )
```

profile of v0, /device:TPU:0, one launch (start us, length us, event | category | flops | bytes accessed | tf_op | source)
XLA Modules:
  0.0 166.7 jit_solution(1666170860876456033)
XLA Ops:
  6.5 0.0 copy-start
  6.5 1.3 convert_reduce_fusion
  7.9 0.1 copy.60
  8.0 1.3 multiply_reduce_fusion
  9.3 1.9 %copy.42 = f32[4,38,1024]{2,1,0:T(8,128)} copy(bf16[4,38,1024]{2,0,1:T(4,128)(2,1)} %param.8) | data formatting | bytes 933888 | tf_op jit(solution)/shard_map/convert_element_type | solution.py:119
  11.2 0.1 div.17
  11.3 0.1 copy.61
  11.4 0.1 rsqrt.12
  11.4 2.0 %reshape.120 = f32[152,1024]{1,0:T(8,128)} reshape(f32[4,38,1024]{2,1,0:T(8,128)} %copy.42) | data formatting | bytes 1245184 | tf_op jit(solution)/shard_map/convert_element_type | solution.py:119
  13.4 2.6 %convolution_convert_fusion = bf16[152,1536]{1,0:T(8,128)(2,1)} fusion(bf16[1024,1536]{1,0:T(8,128)(2,1)S(1)} %copy-done, f32[152,1024]{1,0:T(8,128)} %reshape.120, f32[1024]{0:T(1024)} %param.11, f32[1024]{0:T(1024)} %param.10, f32[152]{0:T(256)S(1)} %rsqrt.12, f32[152]{0:T(256)S(1)} %div.17), kind=kOutput, calls=%fused_computation.22 | convolution fusion | flops 479162368 | bytes 4244672 | tf_op jit(solution)/shard_map/dot_general | solution.py:93
  16.1 2.4 %reshape.115 = bf16[152,3,8,64]{3,2,1,0:T(8,128)(2,1)} reshape(bf16[152,1536]{1,0:T(8,128)(2,1)} %convolution_convert_fusion) | data formatting | bytes 933888 | tf_op jit(solution)/shard_map/reshape | solution.py:97
  18.4 2.8 %copy.46 = bf16[152,3,8,64]{0,3,1,2:T(8,128)(2,1)} copy(bf16[152,3,8,64]{3,2,1,0:T(8,128)(2,1)} %reshape.115) | data formatting | bytes 933888 | tf_op jit(solution)/shard_map/reshape | solution.py:97
  21.3 26.5 %all_to_all.33 = bf16[152,3,8,64]{0,3,1,2:T(8,128)(2,1)S(1)} all-to-all(bf16[152,3,8,64]{0,3,1,2:T(8,128)(2,1)} %copy.46), channel_id=1, replica_groups=mesh['frame'=4,'space'=8] {'frame'}, dimensions={2} | all-to-all | bytes 933888 | tf_op jit(solution)/shard_map/all_to_all | solution.py:98
  47.7 1.5 copy.47
  49.2 2.7 %all_to_all.27 = bf16[608,3,2,64]{0,3,2,1:T(8,128)(2,1)} reshape(bf16[4,152,3,2,64]{1,0,4,3,2:T(4,128)(2,1)} %copy.47) | data formatting | bytes 933888 | tf_op jit(solution)/shard_map/all_to_all | solution.py:98
  51.9 1.8 %fusion.20 = (bf16[608,1,2,64]{0,3,2,1:T(8,128)(2,1)}, bf16[608,2,64]{0,2,1:T(8,128)(2,1)S(1)}, bf16[608,1,2,64]{0,3,2,1:T(8,128)(2,1)S(1)}) fusion(bf16[608,3,2,64]{0,3,2,1:T(8,128)(2,1)} %all_to_all.27), kind=kLoop, calls=%fused_computation.40 | loop fusion | bytes 933888 | tf_op jit(solution)/shard_map/slice | solution.py:102
  53.7 1.7 %copy.49 = bf16[608,128]{1,0:T(8,128)(2,1)} copy(bf16[608,128]{0,1:T(8,128)(2,1)} %bitcast.69) | data formatting | bytes 311296 | tf_op jit(solution)/shard_map/reshape;squeeze | solution.py:102
  55.4 0.0 all-gather.5.cloned.1.call-update
  55.4 0.0 all-gather.3.cloned.1.call-start
  55.4 0.8 copy.48
  56.2 0.0 all-gather.3.cloned.1.call-update
  57.0 0.0 copy-done.4
  57.0 0.6 dynamic-slice
  58.3 8.1 %all-reduce = s32[32]{0:T(128)S(1)} all-reduce(s32[32]{0:T(128)S(1)} %broadcast_dynamic-update-slice_fusion), channel_id=1, replica_groups=mesh['frame'=4,'space'=8] {'space'}, use_global_device_ids=true, to_apply=%add | all-reduce | flops 32 | bytes 256
  66.4 0.1 reshape.114
  66.5 12.4 %all-gather.5.cloned.1.call-done = bf16[4864,128]{1,0:T(8,128)(2,1)} async-done(((bf16[608,128]{1,0:T(8,128)(2,1)}), bf16[4864,128]{1,0:T(8,128)(2,1)}) %all-gather.5.cloned.1.call-update) | async-done | bytes 1245200 | tf_op jit(solution)/shard_map/all_gather | solution.py:109
  78.8 26.1 %all-gather.3.cloned.1.call-done = bf16[4864,128]{1,0:T(8,128)(2,1)} async-done(((bf16[608,128]{1,0:T(8,128)(2,1)}), bf16[4864,128]{1,0:T(8,128)(2,1)}) %all-gather.3.cloned.1.call-update) | async-done | bytes 1245200 | tf_op jit(solution)/shard_map/all_gather | solution.py:108
  105.0 32.1 %while.15 = (s32[]{:T(128)}, f32[2,608]{1,0:T(2,128)S(1)}, f32[2,608]{1,0:T(2,128)S(1)}, f32[2,608,64]{1,2,0:T(8,128)}, s32[2,16]{1,0:T(2,128)S(1)}, /*index=5*/...) while((s32[]{:T(128)}, f32[2,608]{1,0:T(2,128)S(1)}, ...), condition=%wide.region_5.6_spmd.clone, body=%wide.region_2.5_spmd.clone.sunk | while | flops 789841920 | bytes 47565588 | solution.py:72
  105.0 0.1 iota_compare_fusion.3
  105.0 0.1 broadcast_in_dim.99
  105.1 0.1 broadcast_in_dim.100
  105.3 2.4 %constant_dynamic-slice_fusion.4 = (bf16[1,2432,128]{2,1,0:T(8,128)(2,1)}, bf16[1,2432,128]{2,1,0:T(8,128)(2,1)}) fusion(bf16[2,2432,128]{2,1,0:T(8,128)(2,1)} %get-tuple-element.222, s32[]{:T(128)S(6)} %copy.73, bf16[2,2432,128]{2,1,0:T(8,128)(2,1)} %get-tuple-element.220), kind=kLoop, calls=%fused_computation.16.clone.1 | loop fusion | bytes 2490372 | tf_op jit(solution)/shard_map/while/body/jit(dynamic_index_in_dim)/dynamic_slice | solution.py:72
  107.7 2.1 %copy.66 = bf16[1,2432,128]{1,2,0:T(8,128)(2,1)} copy(bf16[1,2432,128]{2,1,0:T(8,128)(2,1)} %get-tuple-element.189) | data formatting | bytes 1245184 | tf_op jit(solution)/shard_map/while/body/jit(dynamic_index_in_dim)/dynamic_slice | solution.py:72
  109.8 2.1 %copy.67 = bf16[1,2432,128]{1,2,0:T(8,128)(2,1)} copy(bf16[1,2432,128]{2,1,0:T(8,128)(2,1)} %get-tuple-element.193) | data formatting | bytes 1245184 | tf_op jit(solution)/shard_map/while/body/jit(dynamic_index_in_dim)/dynamic_slice | solution.py:72
  111.9 3.1 %bitcast_reduce_fusion.2 = (f32[2,608]{1,0:T(2,128)S(1)}, f32[2,2432,608]{1,2,0:T(8,128)S(1)}) fusion(pred[2432]{0:T(1024)(128)(4,1)S(1)} %broadcast_in_dim.100, bf16[2432,2,64]{0,2,1:T(8,128)(2,1)} %bitcast.60, bf16[608,2,64]{0,2,1:T(8,128)(2,1)S(1)} %get-tuple-element.221), kind=kOutput, calls=%fused_computation.1.clone.1 | convolution fusion | flops 387406656 | bytes 12614784 | tf_op jit(solution)/shard_map/while/body/eval_jaxpr/qhd,khd->hqk/dot_general | solution.py:34
  115.1 2.5 %fusion.42 = f32[2,608]{1,0:T(2,128)S(1)} fusion(f32[2,2432,608]{1,2,0:T(8,128)S(1)} %get-tuple-element.191, f32[2,608]{1,0:T(2,128)S(1)} %fusion.41, pred[2432]{0:T(1024)(128)(4,1)S(1)} %broadcast_in_dim.100), kind=kLoop, calls=%fused_computation.5.clone.1 | loop fusion | flops 11828032 | bytes 11841408 | tf_op jit(solution)/shard_map/while/body/eval_jaxpr/reduce_sum | solution.py:41
  117.6 0.0 copy-done.1
  117.6 0.0 copy-done.2
  117.6 2.6 %fusion.44 = f32[2,608,64]{1,2,0:T(8,128)S(1)} fusion(bf16[2432,2,64]{0,2,1:T(8,128)(2,1)S(1)} %bitcast.61, f32[2,2432,608]{1,2,0:T(8,128)S(1)} %get-tuple-element.191, f32[2,608]{1,0:T(2,128)S(1)} %fusion.41, pred[2432]{0:T(1024)(128)(4,1)S(1)} %broadcast_in_dim.100, f32[2,608,64]{1,2,0:T(8,128)S(1)} %copy-done.2, ...), kind=kOutput, calls=%fused_computation.8.clone.1 | convolution fusion | flops 390598656 | bytes 13086593 | tf_op jit(solution)/shard_map/while/body/eval_jaxpr/hqk,khd->hqd/dot_general | solution.py:42
  120.3 0.0 copy-start.3
  120.3 0.7 copy-done.3
  121.0 0.1 iota_compare_fusion.3
  121.1 0.1 broadcast_in_dim.99
  121.2 0.1 broadcast_in_dim.100
  121.3 2.4 %constant_dynamic-slice_fusion.4 = (bf16[1,2432,128]{2,1,0:T(8,128)(2,1)}, bf16[1,2432,128]{2,1,0:T(8,128)(2,1)}) fusion(bf16[2,2432,128]{2,1,0:T(8,128)(2,1)} %get-tuple-element.222, s32[]{:T(128)S(6)} %copy.73, bf16[2,2432,128]{2,1,0:T(8,128)(2,1)} %get-tuple-element.220), kind=kLoop, calls=%fused_computation.16.clone.1 | loop fusion | bytes 2490372 | tf_op jit(solution)/shard_map/while/body/jit(dynamic_index_in_dim)/dynamic_slice | solution.py:72
  123.7 2.1 %copy.66 = bf16[1,2432,128]{1,2,0:T(8,128)(2,1)} copy(bf16[1,2432,128]{2,1,0:T(8,128)(2,1)} %get-tuple-element.189) | data formatting | bytes 1245184 | tf_op jit(solution)/shard_map/while/body/jit(dynamic_index_in_dim)/dynamic_slice | solution.py:72
  125.9 2.1 %copy.67 = bf16[1,2432,128]{1,2,0:T(8,128)(2,1)} copy(bf16[1,2432,128]{2,1,0:T(8,128)(2,1)} %get-tuple-element.193) | data formatting | bytes 1245184 | tf_op jit(solution)/shard_map/while/body/jit(dynamic_index_in_dim)/dynamic_slice | solution.py:72
  128.0 3.1 %bitcast_reduce_fusion.2 = (f32[2,608]{1,0:T(2,128)S(1)}, f32[2,2432,608]{1,2,0:T(8,128)S(1)}) fusion(pred[2432]{0:T(1024)(128)(4,1)S(1)} %broadcast_in_dim.100, bf16[2432,2,64]{0,2,1:T(8,128)(2,1)} %bitcast.60, bf16[608,2,64]{0,2,1:T(8,128)(2,1)S(1)} %get-tuple-element.221), kind=kOutput, calls=%fused_computation.1.clone.1 | convolution fusion | flops 387406656 | bytes 12614784 | tf_op jit(solution)/shard_map/while/body/eval_jaxpr/qhd,khd->hqk/dot_general | solution.py:34
  131.1 2.5 %fusion.42 = f32[2,608]{1,0:T(2,128)S(1)} fusion(f32[2,2432,608]{1,2,0:T(8,128)S(1)} %get-tuple-element.191, f32[2,608]{1,0:T(2,128)S(1)} %fusion.41, pred[2432]{0:T(1024)(128)(4,1)S(1)} %broadcast_in_dim.100), kind=kLoop, calls=%fused_computation.5.clone.1 | loop fusion | flops 11828032 | bytes 11841408 | tf_op jit(solution)/shard_map/while/body/eval_jaxpr/reduce_sum | solution.py:41
  133.7 2.6 %fusion.44 = f32[2,608,64]{1,2,0:T(8,128)S(1)} fusion(bf16[2432,2,64]{0,2,1:T(8,128)(2,1)S(1)} %bitcast.61, f32[2,2432,608]{1,2,0:T(8,128)S(1)} %get-tuple-element.191, f32[2,608]{1,0:T(2,128)S(1)} %fusion.41, pred[2432]{0:T(1024)(128)(4,1)S(1)} %broadcast_in_dim.100, f32[2,608,64]{1,2,0:T(8,128)S(1)} %copy-done.2, ...), kind=kOutput, calls=%fused_computation.8.clone.1 | convolution fusion | flops 390598656 | bytes 13086593 | tf_op jit(solution)/shard_map/while/body/eval_jaxpr/hqk,khd->hqd/dot_general | solution.py:42
  136.4 0.7 copy-done.3
  137.1 1.7 divide_convert_fusion
  138.7 1.1 copy.54
  139.9 0.9 reshape.128
  140.7 4.6 %all-to-all-start.1 = ((bf16[4,2,9728]{2,1,0:T(2,128)(2,1)}), bf16[4,2,9728]{2,1,0:T(2,128)(2,1)}, u32[]{:S(2)}, u32[]{:S(2)}) async-start(bf16[4,2,9728]{2,1,0:T(2,128)(2,1)} %reshape.128), calls=%async_computation.1 | async-start | bytes 311296 | tf_op jit(solution)/shard_map/all_to_all | solution.py:117
  145.3 0.1 broadcast_in_dim.58
  145.4 0.1 broadcast_in_dim.59
  145.5 6.6 %all-to-all-done.1 = bf16[4,2,9728]{2,1,0:T(2,128)(2,1)} async-done(((bf16[4,2,9728]{2,1,0:T(2,128)(2,1)}), bf16[4,2,9728]{2,1,0:T(2,128)(2,1)}, u32[]{:S(2)}, u32[]{:S(2)}) %all-to-all-start.1) | async-done | bytes 155680 | tf_op jit(solution)/shard_map/all_to_all | solution.py:117
  152.1 1.2 reshape.129
  153.3 0.9 copy.63
  154.2 1.2 reshape.118
  155.4 2.5 %fusion.15 = bf16[152,1024]{1,0:T(8,128)(2,1)} fusion(f32[152,1024]{1,0:T(8,128)} %reshape.120, bf16[152,512]{1,0:T(8,128)(2,1)S(1)} %reshape.118, bf16[512,1024]{1,0:T(8,128)(2,1)} %param.13, pred[152]{0:T(512)(128)(4,1)S(1)} %broadcast_in_dim.59), kind=kOutput, calls=%fused_computation.25 | convolution fusion | flops 159850496 | bytes 2138264 | tf_op jit(solution)/shard_map/dot_general | solution.py:119
  157.9 1.1 reshape.119
  158.9 1.0 copy.56
  (26 shorter events, 0.2 us)
Async XLA Ops:
  6.5 6.9 %copy-start = (bf16[1024,1536]{1,0:T(8,128)(2,1)S(1)}, bf16[1024,1536]{1,0:T(8,128)(2,1)}, u32[]{:S(2)}) copy-start(bf16[1024,1536]{1,0:T(8,128)(2,1)} %param.12) | copy-start | bytes 9437188
  6.5 50.4 %copy-start.4 = (u32[32]{0:T(128)S(1)}, u32[32]{0:T(128)}, u32[]{:S(2)}) copy-start(u32[32]{0:T(128)} %constant.36) | copy-start | bytes 388
  6.5 72.3 %all-gather.5.cloned.1.call-start = ((), (), s32[]{:S(2)}) async-start(), calls=%async_computation.3 | async-start | bytes 1400832 | tf_op jit(solution)/shard_map/all_gather | solution.py:109
  55.4 49.6 %all-gather.3.cloned.1.call-start = ((), (), s32[]{:S(2)}) async-start(), calls=%async_computation.2 | async-start | bytes 1400832 | tf_op jit(solution)/shard_map/all_gather | solution.py:108
  111.9 5.7 %copy-start.1 = (bf16[1,2432,128]{1,2,0:T(8,128)(2,1)S(1)}, bf16[1,2432,128]{1,2,0:T(8,128)(2,1)}, u32[]{:S(2)}) copy-start(bf16[1,2432,128]{1,2,0:T(8,128)(2,1)} %copy.67) | copy-start | bytes 1867780 | tf_op jit(solution)/shard_map/while
  111.9 5.7 %copy-start.2 = (f32[2,608,64]{1,2,0:T(8,128)S(1)}, f32[2,608,64]{1,2,0:T(8,128)}, u32[]{:S(2)}) copy-start(f32[2,608,64]{1,2,0:T(8,128)} %get-tuple-element.208) | copy-start | bytes 933892 | tf_op jit(solution)/shard_map/while
  120.3 0.7 copy-start.3
  128.0 5.7 %copy-start.1 = (bf16[1,2432,128]{1,2,0:T(8,128)(2,1)S(1)}, bf16[1,2432,128]{1,2,0:T(8,128)(2,1)}, u32[]{:S(2)}) copy-start(bf16[1,2432,128]{1,2,0:T(8,128)(2,1)} %copy.67) | copy-start | bytes 1867780 | tf_op jit(solution)/shard_map/while
  128.0 5.7 %copy-start.2 = (f32[2,608,64]{1,2,0:T(8,128)S(1)}, f32[2,608,64]{1,2,0:T(8,128)}, u32[]{:S(2)}) copy-start(f32[2,608,64]{1,2,0:T(8,128)} %get-tuple-element.208) | copy-start | bytes 933892 | tf_op jit(solution)/shard_map/while
  136.3 0.7 copy-start.3
  140.7 11.3 %all-to-all-start.1 = ((bf16[4,2,9728]{2,1,0:T(2,128)(2,1)}), bf16[4,2,9728]{2,1,0:T(2,128)(2,1)}, u32[]{:S(2)}, u32[]{:S(2)}) async-start(bf16[4,2,9728]{2,1,0:T(2,128)(2,1)} %reshape.128), calls=%async_computation.1 | async-start | bytes 311296 | tf_op jit(solution)/shard_map/all_to_all | solution.py:117
Sparse Core Ops, SparseCore 0:
  55.5 23.2 all-gather.4
  80.7 24.1 all-gather.2
where the time goes:
time: 168 us; the launch traced here: 167 us
  waiting for transfers between devices  45.1 us (27%)
  local copies, waits for them, and re-layouts  41.4 us (25%)
  blocking collectives  34.5 us (21%)
  matrix products  16.6 us (10%)
  between operations  14.8 us (9%)
  other arithmetic  9.53 us (6%)
  starting transfers between devices  4.64 us (3%)
    all_to_all x1, blocking collectives, on_device(): lax.all_to_all(stacked, 'frame', split_axis=2, concat_axis=0, tiled=True)  26.5 us
    all_gather x1, waiting for transfers between devices, on_device(): lax.all_gather(key_local, 'space', axis=0, tiled=True)  26.1 us
    dynamic_slice x6, local copies, waits for them, and re-layouts, fold_masked(): lax.scan(step_group, carry, (key_groups, value_groups, count_groups))  13.3 us
    all_gather x1, waiting for transfers between devices, on_device(): lax.all_gather(value_local, 'space', axis=0, tiled=True)  12.4 us
    unnamed x1, blocking collectives  8.09 us
    all_to_all x1, waiting for transfers between devices, on_device(): lax.all_to_all(attended, 'frame', split_axis=0, concat_axis=1, tiled=True)  6.57 us
    dot_general x2, matrix products, attend(): jnp.einsum('qhd,khd->hqk', query_heads, key_heads, preferred_element_type...  6.27 us
    dot_general x2, matrix products, attend(): jnp.einsum('hqk,khd->hqd', weights.astype(jnp.bfloat16), value_heads, pre...  5.28 us
  transfers between devices with their start and end apart: 3, of which 3 were waited for; matrix products, arithmetic and copies ran while one was open for 1% of the time, Pallas kernels for 0%

commit v1 on v0

v1 whole, which is shorter than its diff:
```python
import functools

import jax
import jax.numpy as jnp
from jax import lax
from jax.experimental import pallas as pl
from jax.experimental.pallas import tpu as pltpu
from jax.sharding import PartitionSpec as P

HEADS = 8
EPSILON = 1e-06
NEG_FILL = -1e30
SUB = 16


def flip(index, bit):
    return index + bit - 2 * bit * lax.rem(lax.div(index, bit), 2)


def bits_of(number):
    return [1 << i for i in range(number.bit_length()) if (number >> i) & 1]


def layer_kernel(
    frames, spaces, slots, times, rows, head_size,
    tok_ref, cnt_ref, gain_ref, bias_ref, wqkv_hbm, wout_hbm, out_ref,
    nrm, wqkv, wout, sbuf, qall, kbuf, vbuf, qexp, vext, acc, best, obuf, abuf,
    w_sem, z_send, z_recv, r_send, r_recv, s_send, s_recv, o_send, o_recv,
):
    f = lax.axis_index("frame")
    s = lax.axis_index("space")
    chips = spaces // 2
    chip_bits = bits_of(chips - 1)
    core_peer = flip(s, 1)
    width_in = kbuf.shape[-1]
    heads = width_in // head_size
    inner = frames * width_in
    live_rows = slots * times

    def frame_at(d):
        return lax.rem(f + d, frames)

    def chip_peer(bit):
        return flip(s, 2 * bit)

    w_copies = [
        pltpu.make_async_copy(wqkv_hbm.at[:, pl.ds(t * inner, inner)], wqkv.at[t], w_sem.at[t])
        for t in range(3)
    ]
    w_copies.append(pltpu.make_async_copy(wout_hbm, wout, w_sem.at[3]))
    for copy in w_copies:
        copy.start()

    barrier = pltpu.get_barrier_semaphore()
    peers = [{"frame": frame_at(d), "space": s} for d in range(1, frames)]
    peers += [{"frame": f, "space": chip_peer(b)} for b in chip_bits]
    peers += [{"frame": f, "space": core_peer}]
    for peer in peers:
        pl.semaphore_signal(barrier, inc=1, device_id=peer, device_id_type=pl.DeviceIdType.MESH)

    count = cnt_ref[0]
    gain = gain_ref[...]
    bias = bias_ref[...]
    first32 = tok_ref[0].astype(jnp.float32)
    for v in range(slots):
        values32 = first32
        if v:
            values32 = jnp.where(v < count, tok_ref[v].astype(jnp.float32), first32)
        center = values32 - jnp.mean(values32, axis=-1, keepdims=True)
        spread = jnp.mean(center * center, axis=-1, keepdims=True)
        normed = center * lax.rsqrt(spread + EPSILON) * gain + bias
        nrm[pl.ds(v * times, times), :] = normed
        if v == 0 and rows > live_rows:
            nrm[pl.ds(live_rows, rows - live_rows), :] = normed[: rows - live_rows]
    normed16 = nrm[...].astype(jnp.bfloat16)

    def z_copy(t, d):
        g = frame_at(d)
        dst = (qall.at[f], kbuf.at[0, 0, f], vbuf.at[0, 0, f])[t]
        return pltpu.make_async_remote_copy(
            src_ref=sbuf.at[t, g], dst_ref=dst,
            send_sem=z_send.at[t, d], recv_sem=z_recv.at[t, frames - d],
            device_id={"frame": g, "space": s}, device_id_type=pl.DeviceIdType.MESH,
        )

    def z_wait(t, d):
        g = frame_at(d)
        dst = (qall.at[g], kbuf.at[0, 0, g], vbuf.at[0, 0, g])[t]
        pltpu.make_async_remote_copy(
            src_ref=sbuf.at[t, g], dst_ref=dst,
            send_sem=z_send.at[t, d], recv_sem=z_recv.at[t, d],
            device_id={"frame": g, "space": s}, device_id_type=pl.DeviceIdType.MESH,
        ).wait_recv()

    bufs = (None, kbuf, vbuf)

    def relay(t, p, bit, d):
        g = frame_at(d)
        return pltpu.make_async_remote_copy(
            src_ref=bufs[t].at[p, 0, g], dst_ref=bufs[t].at[p ^ bit, 0, g],
            send_sem=r_send.at[t - 1, p ^ bit, d], recv_sem=r_recv.at[t - 1, p ^ bit, d],
            device_id={"frame": f, "space": chip_peer(bit)},
            device_id_type=pl.DeviceIdType.MESH,
        )

    def share(t, p, d):
        g = frame_at(d)
        return pltpu.make_async_remote_copy(
            src_ref=bufs[t].at[p, 0, g], dst_ref=bufs[t].at[p, 1, g],
            send_sem=s_send.at[t - 1, p, d], recv_sem=s_recv.at[t - 1, p, d],
            device_id={"frame": f, "space": core_peer},
            device_id_type=pl.DeviceIdType.MESH,
        )

    def path_bit(t, p):
        return bits_of(p)[0] if t == 1 else bits_of(p)[-1]

    def onward(t, p, d):
        copies = []
        for bit in chip_bits:
            if not p & bit and path_bit(t, p ^ bit) == bit:
                copies.append(relay(t, p, bit, d))
        copies.append(share(t, p, d))
        return copies

    in_flight = []

    def launch(copies):
        for copy in copies:
            copy.start()
            in_flight.append(copy)

    scaling = head_size ** (-0.5)
    row_ids = lax.broadcasted_iota(jnp.int32, (rows, 1), 0)
    count32 = count.astype(jnp.float32)
    for t in range(3):
        w_copies[t].wait()
        product = jnp.dot(normed16, wqkv[t], preferred_element_type=jnp.float32)
        if t == 0:
            product = product.astype(jnp.bfloat16).astype(jnp.float32) * scaling
        if t == 2:
            product = jnp.where(row_ids < live_rows, product, count32)
        product = product.astype(jnp.bfloat16)
        for g in range(frames):
            sbuf[t, g] = product[:, g * width_in:(g + 1) * width_in]
        if t == 0:
            qall[f] = sbuf[t, f]
        else:
            bufs[t][0, 0, f] = sbuf[t, f]
        if t == 0:
            pl.semaphore_wait(barrier, len(peers))
        launch([z_copy(t, d) for d in range(1, frames)])
        if t:
            launch(onward(t, 0, 0))

    for d in range(1, frames):
        z_wait(0, d)
    lane_head = lax.broadcasted_iota(jnp.int32, (1, width_in), 1)
    for h in range(heads):
        mine = (lane_head >= h * head_size) & (lane_head < (h + 1) * head_size)
        for g in range(frames):
            block = qall[g].astype(jnp.float32)
            qexp[pl.ds((h * frames + g) * rows, rows), :] = jnp.where(mine, block, 0.0).astype(
                jnp.bfloat16
            )

    for t in (1, 2):
        for d in range(1, frames):
            z_wait(t, d)
            launch(onward(t, 0, d))

    total_rows = heads * frames * rows
    keys = frames * rows
    step_rows = 2 * rows
    steps = total_rows // step_rows
    key_ids = lax.broadcasted_iota(jnp.int32, (rows, width_in), 0).astype(jnp.float32)

    def fold(p, j, first):
        for g in range(frames):
            values = vbuf[p, j, g].astype(jnp.float32)
            limit = values[rows - 8:rows][0:1] * float(times)
            live = key_ids < limit
            vext[pl.ds(g * rows, rows), 0:width_in] = jnp.where(live, values, 0.0).astype(
                jnp.bfloat16
            )
            vext[pl.ds(g * rows, rows), width_in:2 * width_in] = jnp.where(
                live, 1.0, 0.0
            ).astype(jnp.bfloat16)

        def step(i, carry):
            part = pl.ds(pl.multiple_of(i * step_rows, SUB), step_rows)
            scores = lax.dot_general(
                qexp[part, :], kbuf[p, j].reshape(keys, width_in),
                (((1,), (1,)), ((), ())), preferred_element_type=jnp.float32,
            )
            top = jnp.max(scores, axis=-1, keepdims=True)
            if not first:
                old = best[part, :][:, 0:1]
                top = jnp.maximum(top, old)
            weights = jnp.exp(scores - top).astype(jnp.bfloat16)
            added = jnp.dot(weights, vext[...], preferred_element_type=jnp.float32)
            if first:
                acc[part, :] = added
            else:
                acc[part, :] = acc[part, :] * jnp.exp(old - top) + added
            best[part, :] = jnp.broadcast_to(top, (step_rows, best.shape[1]))
            return carry

        lax.fori_loop(0, steps, step, 0, unroll=2 if steps % 2 == 0 else 1)

    fold(0, 0, True)

    def arrive(p):
        for t in (1, 2):
            for d in range(frames):
                relay(t, p ^ path_bit(t, p), path_bit(t, p), d).wait_recv()
                launch(onward(t, p, d))

    def arrive_shared(p):
        for t in (1, 2):
            for d in range(frames):
                share(t, p, d).wait_recv()

    order = sorted(range(1, chips), key=lambda p: (len(bits_of(p)), p))
    waves = {}
    for p in order:
        waves.setdefault(len(bits_of(p)), []).append(p)
    pending = [0]
    for level in sorted(waves):
        for p in waves[level]:
            arrive(p)
        for p in pending:
            arrive_shared(p)
            fold(p, 1, False)
        for p in waves[level]:
            fold(p, 0, False)
        pending = waves[level]
    for p in pending:
        arrive_shared(p)
        fold(p, 1, False)

    def o_copy(d, dst_frame):
        g = frame_at(d)
        return pltpu.make_async_remote_copy(
            src_ref=obuf.at[g], dst_ref=abuf.at[dst_frame],
            send_sem=o_send.at[d], recv_sem=o_recv.at[frames - d],
            device_id={"frame": g, "space": s}, device_id_type=pl.DeviceIdType.MESH,
        )

    for g in range(frames):
        joined = None
        for h in range(heads):
            part = pl.ds((h * frames + g) * rows, rows)
            value = acc[part, 0:width_in] / acc[part, width_in:2 * width_in]
            if joined is None:
                joined = value
            else:
                joined = jnp.where(lane_head < h * head_size, joined, value)
        obuf[g] = joined.astype(jnp.bfloat16)
    abuf[f] = obuf[f]
    launch([o_copy(d, f) for d in range(1, frames)])
    w_copies[3].wait()
    for d in range(1, frames):
        g = frame_at(d)
        pltpu.make_async_remote_copy(
            src_ref=obuf.at[g], dst_ref=abuf.at[g],
            send_sem=o_send.at[d], recv_sem=o_recv.at[d],
            device_id={"frame": g, "space": s}, device_id_type=pl.DeviceIdType.MESH,
        ).wait_recv()
    attended = jnp.concatenate([abuf[g] for g in range(frames)], axis=1)
    nrm[...] = jnp.dot(attended, wout[...], preferred_element_type=jnp.float32)
    for v in range(slots):
        mixed = tok_ref[v].astype(jnp.float32) + nrm[pl.ds(v * times, times), :]
        out_ref[v] = jnp.where(v < count, mixed, 0.0).astype(jnp.bfloat16)
    for copy in in_flight:
        copy.wait_send()


def on_device(frames, spaces, tokens, tube_count, ln_gain, ln_bias, w_qkv, w_out):
    slots, times, width = tokens.shape
    inner = w_out.shape[0]
    head_size = inner // HEADS
    width_in = inner // frames
    rows = -(-(slots * times + 1) // SUB) * SUB
    chips = spaces // 2
    heads = width_in // head_size
    total_rows = heads * frames * rows
    bf16, f32 = jnp.bfloat16, jnp.float32
    vmem = pl.BlockSpec(memory_space=pltpu.VMEM)
    hbm = pl.BlockSpec(memory_space=pl.ANY)
    dma = pltpu.SemaphoreType.DMA
    return pl.pallas_call(
        functools.partial(layer_kernel, frames, spaces, slots, times, rows, head_size),
        out_shape=jax.ShapeDtypeStruct(tokens.shape, bf16),
        in_specs=[vmem, pl.BlockSpec(memory_space=pltpu.SMEM), vmem, vmem, hbm, hbm],
        out_specs=vmem,
        scratch_shapes=[
            pltpu.VMEM((rows, width), f32),
            pltpu.VMEM((3, width, inner), bf16),
            pltpu.VMEM((inner, width), bf16),
            pltpu.VMEM((3, frames, rows, width_in), bf16),
            pltpu.VMEM((frames, rows, width_in), bf16),
            pltpu.VMEM((chips, 2, frames, rows, width_in), bf16),
            pltpu.VMEM((chips, 2, frames, rows, width_in), bf16),
            pltpu.VMEM((total_rows, width_in), bf16),
            pltpu.VMEM((frames * rows, 2 * width_in), bf16),
            pltpu.VMEM((total_rows, 2 * width_in), f32),
            pltpu.VMEM((total_rows, 128), f32),
            pltpu.VMEM((frames, rows, width_in), bf16),
            pltpu.VMEM((frames, rows, width_in), bf16),
            dma((4,)),
            dma((3, frames)), dma((3, frames)),
            dma((2, chips, frames)), dma((2, chips, frames)),
            dma((2, chips, frames)), dma((2, chips, frames)),
            dma((frames,)), dma((frames,)),
        ],
        compiler_params=pltpu.CompilerParams(
            collective_id=0, has_side_effects=True, vmem_limit_bytes=56 * 1024 * 1024
        ),
    )(tokens, tube_count, ln_gain.reshape(1, width), ln_bias.reshape(1, width), w_qkv, w_out)


def solution(mesh):
    in_specs = (P("space", "frame", None), P("space"), P(), P(), P(), P())
    out_specs = P("space", "frame", None)
    body = functools.partial(on_device, mesh.shape["frame"], mesh.shape["space"])
    return jax.shard_map(
        body, mesh=mesh, in_specs=in_specs, out_specs=out_specs, check_vma=False
    )
```

time: 168 us -> 50.1 us (0.30)
  Pallas kernels: 0 us -> 45.5 us
  waiting for transfers between devices: 45.1 us -> 0 us
  local copies, waits for them, and re-layouts: 41.4 us -> 3.71 us
  blocking collectives: 34.5 us -> 0 us
  matrix products: 16.6 us -> 0 us
  between operations: 14.8 us -> 0.66 us
  other arithmetic: 9.53 us -> 0 us
  starting transfers between devices: 4.64 us -> 0 us
    pallas_call x0 -> x1, Pallas kernels: none -> 45.5 us  [on_device(): pl.pallas_call(functools.partial(layer_kernel, frames, spaces, slots, tim...]
    all_gather x2 -> x0, waiting for transfers between devices: 38.5 us -> none  [the longest x1 26.1 us: on_device(): lax.all_gather(key_local, 'space', axis=0, tiled=True)]
    all_to_all x1 -> x0, blocking collectives: 26.5 us -> none  [on_device(): lax.all_to_all(stacked, 'frame', split_axis=2, concat_axis=0, tiled=True)]
    dot_general x6 -> x0, matrix products: 16.6 us -> none  [the longest x2 6.27 us: attend(): jnp.einsum('qhd,khd->hqk', query_heads, key_heads, preferred_element_type...]
    dynamic_slice x6 -> x0, local copies, waits for them, and re-layouts: 13.3 us -> none  [fold_masked(): lax.scan(step_group, carry, (key_groups, value_groups, count_groups))]
    reshape x6 -> x0, local copies, waits for them, and re-layouts: 8.5 us -> none  [the longest x2 5.19 us: on_device(): stacked = projected.reshape(rows_dev, 3, HEADS, head_size)]
    unnamed x1 -> x0, blocking collectives: 8.09 us -> none
    reduce_sum x4 -> x0, other arithmetic: 7.63 us -> none  [the longest x2 5 us: attend(): total_next = total_now * fading + jnp.sum(weights, axis=-1)]
  transfers between devices with their start and end apart: 3 -> 0, of which waited for: 3 -> 0; matrix products, arithmetic and copies ran while one was open for 1% -> 0% of each run, Pallas kernels for 0% -> 0%
where the time goes in v1:
time: 50.1 us; the launch traced here: 49.9 us
  Pallas kernels  45.5 us (91%)
  local copies, waits for them, and re-layouts  3.71 us (7%)
  between operations  0.66 us (1%)
    pallas_call x1, Pallas kernels, on_device(): pl.pallas_call(functools.partial(layer_kernel, frames, spaces, slots, tim...  45.5 us
    pallas_call x1, local copies, waits for them, and re-layouts, on_device(): pl.pallas_call(functools.partial(layer_kernel, frames, spaces, slots, tim...  1.93 us
    unnamed x1, local copies, waits for them, and re-layouts  1.78 us

profile of v1, /device:TPU:0, one launch (start us, length us, event | category | flops | bytes accessed | tf_op | source)
XLA Modules:
  0.0 49.9 jit_solution(10390595145066889398)
XLA Ops:
  0.7 1.8 %copy.7.tok_ref = bf16[4,38,1024]{2,1,0:T(8,128)(2,1)} copy(bf16[4,38,1024]{2,0,1:T(4,128)(2,1)} %param.6) | data formatting | bytes 622592 | tf_op args[0]
  2.4 45.5 %shard_map.64 = bf16[4,38,1024]{2,1,0:T(8,128)(2,1)} custom-call(bf16[4,38,1024]{2,1,0:T(8,128)(2,1)} %copy.7.tok_ref, s32[1]{0:T(128)S(6)} %copy.9.cnt_ref, f32[1,1024]{1,0:T(1,128)} %bitcast.2, f32[1,1024]{1,0:T(1,128)} %bitcast.3, bf16[1024,1536]{1,0:T(8,128)(2,1)} %wqkv_hbm.1, bf16[512,1024]{1,0:T(8,128)(2,1)} %wout_hbm.1), custom_call_target="tpu_custom_call" | custom-call | tf_op jit(solution)/shard_map/pallas_call | solution.py:292
  48.0 1.9 %copy.8 = bf16[4,38,1024]{2,0,1:T(4,128)(2,1)} copy(bf16[4,38,1024]{2,1,0:T(8,128)(2,1)} %shard_map.64) | data formatting | bytes 622592 | tf_op jit(solution)/shard_map/pallas_call | solution.py:292

commit v2 on v1

v2 whole, which is shorter than its diff:
```python
import functools

import jax
import jax.numpy as jnp
from jax import lax
from jax.experimental import pallas as pl
from jax.experimental.pallas import tpu as pltpu
from jax.sharding import PartitionSpec as P

HEADS = 8
EPSILON = 1e-06
SUB = 16


def flip(index, bit):
    return index + bit - 2 * bit * lax.rem(lax.div(index, bit), 2)


def bits_of(number):
    return [1 << i for i in range(number.bit_length()) if (number >> i) & 1]


def layer_kernel(
    frames, spaces, slots, times, rows, head_size,
    tok_ref, cnt_ref, gain_ref, bias_ref, wqkv_hbm, wout_hbm, out_ref,
    nrm, wqkv, wout, qsend, kvsend, qall, kvbuf, qexp, vext, acc, best, obuf, abuf,
    w_sem, z_send, z_recv, r_send, r_recv, s_send, s_recv, o_send, o_recv,
):
    f = lax.axis_index("frame")
    s = lax.axis_index("space")
    chips = spaces // 2
    chip_bits = bits_of(chips - 1)
    core_peer = flip(s, 1)
    width_in = kvbuf.shape[-1]
    heads = width_in // head_size
    inner = frames * width_in
    live_rows = slots * times

    def frame_at(d):
        return lax.rem(f + d, frames)

    def chip_peer(bit):
        return flip(s, 2 * bit)

    w_copies = [
        pltpu.make_async_copy(wqkv_hbm.at[:, pl.ds(t * inner, inner)], wqkv.at[t], w_sem.at[t])
        for t in range(3)
    ]
    w_copies.append(pltpu.make_async_copy(wout_hbm, wout, w_sem.at[3]))
    for t in (1, 2, 0, 3):
        w_copies[t].start()

    barrier = pltpu.get_barrier_semaphore()
    peers = [{"frame": frame_at(d), "space": s} for d in range(1, frames)]
    peers += [{"frame": f, "space": chip_peer(b)} for b in chip_bits]
    peers += [{"frame": f, "space": core_peer}]
    for peer in peers:
        pl.semaphore_signal(barrier, inc=1, device_id=peer, device_id_type=pl.DeviceIdType.MESH)

    count = cnt_ref[0]
    gain = gain_ref[...]
    bias = bias_ref[...]
    slot_live = lax.broadcasted_iota(jnp.int32, (slots, 1), 0) < count
    for i in range(times):
        token32 = tok_ref[i].astype(jnp.float32)
        nrm[pl.ds(i * slots, slots), :] = jnp.where(slot_live, token32, token32[0:1])
    spare = rows - live_rows
    nrm[pl.ds(live_rows, spare), :] = nrm[pl.ds(0, spare), :]
    values32 = nrm[...]
    center = values32 - jnp.mean(values32, axis=-1, keepdims=True)
    spread = jnp.mean(center * center, axis=-1, keepdims=True)
    normed16 = (center * lax.rsqrt(spread + EPSILON) * gain + bias).astype(jnp.bfloat16)

    def remote(src, dst, send_sem, recv_sem, peer):
        return pltpu.make_async_remote_copy(
            src_ref=src, dst_ref=dst, send_sem=send_sem, recv_sem=recv_sem,
            device_id=peer, device_id_type=pl.DeviceIdType.MESH,
        )

    def z_copy(kv, d, home):
        g = frame_at(d)
        src = kvsend.at[g] if kv else qsend.at[g]
        dst = kvbuf.at[home, :, 0, 0] if kv else qall.at[home]
        return src, dst, {"frame": g, "space": s}

    def z_start(kv, d):
        src, dst, peer = z_copy(kv, d, f)
        return remote(src, dst, z_send.at[kv, d], z_recv.at[kv, frames - d], peer)

    def z_wait(kv, d):
        src, dst, peer = z_copy(kv, d, frame_at(d))
        remote(src, dst, z_send.at[kv, d], z_recv.at[kv, d], peer).wait_recv()

    def routes(p):
        low, high = bits_of(p)[0], bits_of(p)[-1]
        return [(2, low)] if low == high else [(0, low), (1, high)]

    def part_of(g, part, p, j):
        return kvbuf.at[g, :, p, j] if part == 2 else kvbuf.at[g, part, p, j]

    def relay(part, p, bit, d):
        g = frame_at(d)
        slot = part % 2
        return remote(
            part_of(g, part, p, 0), part_of(g, part, p ^ bit, 0),
            r_send.at[slot, p ^ bit, d], r_recv.at[slot, p ^ bit, d],
            {"frame": f, "space": chip_peer(bit)},
        )

    def share(p, d):
        g = frame_at(d)
        return remote(
            part_of(g, 2, p, 0), part_of(g, 2, p, 1), s_send.at[p, d], s_recv.at[p, d],
            {"frame": f, "space": core_peer},
        )

    def onward(p, d):
        copies = []
        for bit in chip_bits:
            if not p & bit:
                copies += [relay(part, p, bit, d) for part, by in routes(p ^ bit) if by == bit]
        return copies + [share(p, d)]

    in_flight = []

    def launch(copies):
        for copy in copies:
            copy.start()
            in_flight.append(copy)

    far = sorted(range(1, frames), key=lambda d: (min(d, frames - d), d))
    scaling = head_size ** (-0.5)
    row_ids = lax.broadcasted_iota(jnp.int32, (rows, 1), 0)
    count32 = count.astype(jnp.float32)
    for t in (1, 2, 0):
        w_copies[t].wait()
        product = jnp.dot(normed16, wqkv[t], preferred_element_type=jnp.float32)
        if t == 0:
            product = product.astype(jnp.bfloat16).astype(jnp.float32) * scaling
        if t == 2:
            product = jnp.where(row_ids < live_rows, product, count32)
        product = product.astype(jnp.bfloat16)
        for g in range(frames):
            piece = product[:, g * width_in:(g + 1) * width_in]
            if t == 0:
                qsend[g] = piece
            else:
                kvsend[g, t - 1] = piece
        if t == 0:
            qall[f] = qsend[f]
        else:
            kvbuf[f, t - 1, 0, 0] = kvsend[f, t - 1]
        if t == 2:
            pl.semaphore_wait(barrier, len(peers))
            launch([z_start(1, d) for d in far])
            launch(onward(0, 0))
    launch([z_start(0, d) for d in far])

    lane_head = lax.broadcasted_iota(jnp.int32, (1, width_in), 1)
    keys = spaces * rows
    frame_rows = heads * rows
    row_key = lax.broadcasted_iota(jnp.int32, (rows, width_in), 0)
    slot_key = jnp.where(row_key < live_rows, lax.rem(row_key, slots), slots).astype(jnp.float32)

    def prepare(d):
        g = frame_at(d)
        for p in range(chips):
            for j in range(2):
                values = kvbuf[g, 1, p, j].astype(jnp.float32)
                live = slot_key < values[rows - 8:rows][0:1]
                part = pl.ds((2 * p + j) * rows, rows)
                vext[part, 0:width_in] = jnp.where(live, values, 0.0).astype(jnp.bfloat16)
                vext[part, width_in:2 * width_in] = jnp.where(live, 1.0, 0.0).astype(jnp.bfloat16)

    def fold(d, first, start, count):
        size = count * frame_rows
        part = pl.ds(pl.multiple_of(start * frame_rows, SUB), size)
        scores = lax.dot_general(
            qexp[part, :], kvbuf[frame_at(d), 0].reshape(keys, width_in),
            (((1,), (1,)), ((), ())), preferred_element_type=jnp.float32,
        )
        top = jnp.max(scores, axis=-1, keepdims=True)
        if not first:
            old = best[part, :][:, 0:1]
            top = jnp.maximum(top, old)
        weights = jnp.exp(scores - top).astype(jnp.bfloat16)
        added = jnp.dot(weights, vext[...], preferred_element_type=jnp.float32)
        if first:
            acc[part, :] = added
        else:
            acc[part, :] = acc[part, :] * jnp.exp(old - top) + added
        best[part, :] = jnp.broadcast_to(top, (size, best.shape[1]))

    order = sorted(range(1, chips), key=lambda p: (len(bits_of(p)), p))

    sequence = [0] + far
    levels = len(chip_bits)
    done = set()

    def once(what, n, level=0):
        if n >= len(sequence) or (what, n, level) in done:
            return
        done.add((what, n, level))
        d = sequence[n]
        if what == "frame" and n:
            z_wait(1, d)
            launch(onward(0, d))
        if what == "chip":
            for p in order:
                if len(bits_of(p)) == level:
                    for part, bit in routes(p):
                        relay(part, p ^ bit, bit, d).wait_recv()
                    launch(onward(p, d))
        if what == "core":
            for p in range(chips):
                share(p, d).wait_recv()

    def chip_levels(n, low, high):
        for level in range(low, high + 1):
            once("chip", n, level)

    def o_copy(d, home, arrival):
        g = frame_at(d)
        return remote(
            obuf.at[g], abuf.at[home], o_send.at[d], o_recv.at[arrival], {"frame": g, "space": s}
        )

    def finish(d):
        g = frame_at(d)
        joined = None
        for h in range(heads):
            part = pl.ds(pl.multiple_of(g * frame_rows + h * rows, SUB), rows)
            value = acc[part, 0:width_in] / acc[part, width_in:2 * width_in]
            joined = value if h == 0 else jnp.where(lane_head < h * head_size, joined, value)
        obuf[g] = joined.astype(jnp.bfloat16)
        if d:
            launch([o_copy(d, f, frames - d)])
        else:
            abuf[f] = obuf[f]

    once("frame", 1)
    once("chip", 0, 1)
    once("frame", 2)
    once("chip", 1, 1)
    chip_levels(0, 2, levels)
    for n in range(3, frames):
        once("frame", n)
    chip_levels(1, 2, levels)
    once("chip", 2, 1)
    for d in far:
        z_wait(0, d)
    for h in range(heads):
        mine = (lane_head >= h * head_size) & (lane_head < (h + 1) * head_size)
        for g in range(frames):
            block = qall[g].astype(jnp.float32)
            qexp[pl.ds((g * heads + h) * rows, rows), :] = jnp.where(mine, block, 0.0).astype(
                jnp.bfloat16
            )

    once("core", 0)
    for n in range(frames - 1):
        prepare(sequence[n])
        half = frames // 2
        fold(sequence[n], n == 0, 0, half)
        once("chip", n + 1, 1)
        if n:
            once("chip", n + 2, 1)
            chip_levels(n + 1, 2, levels)
        fold(sequence[n], n == 0, half, frames - half)
        once("frame", n + 3)
        chip_levels(n + 1, 1, levels)
        once("chip", n + 2, 1)
        once("core", n + 1)
    prepare(sequence[-1])
    for d in far[::-1] + [0]:
        fold(sequence[-1], frames == 1, frame_at(d), 1)
        finish(d)

    w_copies[3].wait()
    for d in far:
        o_copy(d, frame_at(d), d).wait_recv()
    attended = jnp.concatenate([abuf[g] for g in range(frames)], axis=1)
    nrm[...] = jnp.dot(attended, wout[...], preferred_element_type=jnp.float32)
    for i in range(times):
        mixed = tok_ref[i].astype(jnp.float32) + nrm[pl.ds(i * slots, slots), :]
        out_ref[i] = jnp.where(slot_live, mixed, 0.0).astype(jnp.bfloat16)
    for copy in in_flight:
        copy.wait_send()


def on_device(frames, spaces, tokens, tube_count, ln_gain, ln_bias, w_qkv, w_out):
    slots, times, width = tokens.shape
    inner = w_out.shape[0]
    head_size = inner // HEADS
    width_in = inner // frames
    rows = -(-(slots * times + 1) // SUB) * SUB
    chips = spaces // 2
    heads = width_in // head_size
    total_rows = heads * frames * rows
    bf16, f32 = jnp.bfloat16, jnp.float32
    vmem = pl.BlockSpec(memory_space=pltpu.VMEM)
    hbm = pl.BlockSpec(memory_space=pl.ANY)
    dma = pltpu.SemaphoreType.DMA
    mixed = pl.pallas_call(
        functools.partial(layer_kernel, frames, spaces, slots, times, rows, head_size),
        out_shape=jax.ShapeDtypeStruct((times, slots, width), bf16),
        in_specs=[vmem, pl.BlockSpec(memory_space=pltpu.SMEM), vmem, vmem, hbm, hbm],
        out_specs=vmem,
        scratch_shapes=[
            pltpu.VMEM((rows, width), f32),
            pltpu.VMEM((3, width, inner), bf16),
            pltpu.VMEM((inner, width), bf16),
            pltpu.VMEM((frames, rows, width_in), bf16),
            pltpu.VMEM((frames, 2, rows, width_in), bf16),
            pltpu.VMEM((frames, rows, width_in), bf16),
            pltpu.VMEM((frames, 2, chips, 2, rows, width_in), bf16),
            pltpu.VMEM((total_rows, width_in), bf16),
            pltpu.VMEM((spaces * rows, 2 * width_in), bf16),
            pltpu.VMEM((total_rows, 2 * width_in), f32),
            pltpu.VMEM((total_rows, 128), f32),
            pltpu.VMEM((frames, rows, width_in), bf16),
            pltpu.VMEM((frames, rows, width_in), bf16),
            dma((4,)),
            dma((2, frames)), dma((2, frames)),
            dma((2, chips, frames)), dma((2, chips, frames)),
            dma((chips, frames)), dma((chips, frames)),
            dma((frames,)), dma((frames,)),
        ],
        compiler_params=pltpu.CompilerParams(
            collective_id=0, has_side_effects=True, vmem_limit_bytes=56 * 1024 * 1024
        ),
    )(
        jnp.transpose(tokens, (1, 0, 2)), tube_count,
        ln_gain.reshape(1, width), ln_bias.reshape(1, width), w_qkv, w_out,
    )
    return jnp.transpose(mixed, (1, 0, 2))


def solution(mesh):
    in_specs = (P("space", "frame", None), P("space"), P(), P(), P(), P())
    out_specs = P("space", "frame", None)
    body = functools.partial(on_device, mesh.shape["frame"], mesh.shape["space"])
    return jax.shard_map(
        body, mesh=mesh, in_specs=in_specs, out_specs=out_specs, check_vma=False
    )
```

time: 50.1 us -> 46.8 us (0.934)
  local copies, waits for them, and re-layouts: 3.71 us -> 1.8 us
  Pallas kernels: 45.5 us -> 44.2 us
    pallas_call x1 -> x0, local copies, waits for them, and re-layouts: 1.93 us -> none  [on_device(): pl.pallas_call(functools.partial(layer_kernel, frames, spaces, slots, tim...]
    pallas_call x1, Pallas kernels: 45.5 us -> 44.2 us  [on_device(): pl.pallas_call(functools.partial(layer_kernel, frames, spaces, slots, tim...]
where the time goes in v2:
time: 46.8 us; the launch traced here: 46.6 us
  Pallas kernels  44.2 us (94%)
  local copies, waits for them, and re-layouts  1.8 us (4%)
  between operations  0.66 us (1%)
    pallas_call x1, Pallas kernels, on_device(): pl.pallas_call(functools.partial(layer_kernel, frames, spaces, slots, tim...  44.2 us
    unnamed x1, local copies, waits for them, and re-layouts  1.8 us

profile of v2, /device:TPU:0, one launch (start us, length us, event | category | flops | bytes accessed | tf_op | source)
XLA Modules:
  0.0 46.6 jit_solution(17070740824202991735)
XLA Ops:
  0.7 44.2 %shard_map.64 = bf16[38,4,1024]{2,1,0:T(4,128)(2,1)} custom-call(bf16[38,4,1024]{2,1,0:T(4,128)(2,1)} %bitcast.5, s32[1]{0:T(128)S(6)} %copy.8.cnt_ref, f32[1,1024]{1,0:T(1,128)} %bitcast.6, f32[1,1024]{1,0:T(1,128)} %bitcast.7, bf16[1024,1536]{1,0:T(8,128)(2,1)} %wqkv_hbm.1, bf16[512,1024]{1,0:T(8,128)(2,1)} %wout_hbm.1), custom_call_target="tpu_custom_call" | custom-call | tf_op jit(solution)/shard_map/pallas_call | solution.py:304
  44.9 1.8 %copy.9 = bf16[4,38,1024]{2,0,1:T(4,128)(2,1)} copy(bf16[4,38,1024]{2,0,1:T(4,128)(2,1)} %bitcast.4) | data formatting | bytes 622592
